TPU v7x, 128 devices: a whole 4x4x4 slice. The times are simulated.
128 devices in a mesh: expert: 8 (over x, core), shard: 16 (over z, y).
Axes of the slice: x: 4, y: 4, z: 4, core: 2. Of those that a mesh axis runs over, the one named last changes fastest.
Arguments:
- tokens: bfloat16 [1024, 4096], P(('expert', 'shard')), may hold values from -6 to 6
- router: bfloat16 [4096, 8], replicated, may hold values from -0.09375 to 0.09375
- expert_ids: int32 [1024, 2], P(('expert', 'shard')), may hold values from 0 to 7, as said below
- w_gate: bfloat16 [8, 4096, 14336], P('expert', None, 'shard'), may hold values from -0.09375 to 0.09375
- w_up: bfloat16 [8, 4096, 14336], P('expert', None, 'shard'), may hold values from -0.09375 to 0.09375
- w_down: bfloat16 [8, 14336, 4096], P('expert', 'shard'), may hold values from -0.046875 to 0.046875
Outputs:
- mixed: bfloat16 [1024, 4096], P(('expert', 'shard'))
Inputs may be any that keep to these rules, and one draw needn't show every extreme that they name: `expert_ids`: each row names 2 different experts. Within the rows of one device no expert is named more than 4 times, and on every device some expert is named exactly 4 times.
All inputs are finite; a program needn't handle non-finite values.
Results may differ from a plain program's by a relative error of at most 0.0074.
Values may be sent and summed in bfloat16 or wider, within the bound.
A program may use at most 128 MiB of HBM per device.

v0:
```python
import jax
import jax.numpy as jnp
from jax import lax
from jax.sharding import PartitionSpec as P


def from_behind(value, axis, steps):
    count = lax.axis_size(axis)
    pairs = [(source, (source + steps) % count) for source in range(count)]
    return lax.ppermute(value, axis, pairs)


def laid_out(blocks, dim):
    blocks = jnp.moveaxis(blocks, 0, dim)
    dims = blocks.shape
    return blocks.reshape(*dims[:dim], dims[dim] * dims[dim + 1], *dims[dim + 2 :])


def work_in_pieces(x, axis, dim, apply, out_dim):
    devices, extent = (lax.axis_size(axis), x.shape[dim])
    count = 2 if extent % 2 == 0 else 1
    gathered, length = ([], extent // count)
    for k in range(count):
        share = lax.slice_in_dim(x, k * length, (k + 1) * length, axis=dim)
        starts = jnp.arange(devices) * extent + k * length
        gathered.append(jax.vmap(apply)(lax.all_gather(share, axis), starts))
    return laid_out(jnp.concatenate(gathered, axis=out_dim + 1), out_dim)


def split_up(x, dim, devices):
    before, after = (x.shape[:dim], x.shape[dim + 1 :])
    return jnp.moveaxis(x.reshape(*before, devices, -1, *after), dim, 0)


def sum_at_owner(x, axis, dim):
    devices = lax.axis_size(axis)
    blocks = lax.all_to_all(split_up(x, dim, devices), axis, 0, 0, tiled=True)
    return jnp.sum(blocks.astype(jnp.float32), axis=0)


def shards(tokens, router, expert_ids, w_gate, w_up, w_down):
    local_tokens = tokens.shape[0]
    width = tokens.shape[1]
    n_experts = router.shape[1]
    slots_per = local_tokens // 2
    half_slots = slots_per // 2
    shadow_gate, shadow_up, shadow_down = from_behind((w_gate, w_up, w_down), "expert", -1)
    logits = jnp.dot(tokens, router, preferred_element_type=jnp.float32)
    chosen = jnp.take_along_axis(logits, expert_ids, axis=1)
    first = 1.0 / (1.0 + jnp.exp(-(chosen[:, 0] - chosen[:, 1])))
    gates = jnp.stack([first, 1.0 - first], axis=1)
    flat_ids = expert_ids.reshape(-1)
    onehot = (flat_ids[:, None] == jnp.arange(n_experts, dtype=jnp.int32)[None, :]).astype(
        jnp.int32
    )
    before = jnp.cumsum(onehot, axis=0) - onehot
    slots = jnp.sum(before * onehot, axis=1)
    positions = flat_ids * slots_per + slots
    token_index = jnp.repeat(jnp.arange(local_tokens, dtype=jnp.int32), expert_ids.shape[1])
    outgoing = jnp.zeros((n_experts * slots_per, width), jnp.bfloat16)
    outgoing = outgoing.at[positions].set(tokens[token_index])
    outgoing = outgoing.reshape(n_experts, half_slots, 2, width)
    even_rows = outgoing[:, :, 0]
    odd_rows = jnp.roll(outgoing[:, :, 1], -1, axis=0)
    sending = jnp.stack([even_rows, odd_rows], axis=0)
    arrived = lax.all_to_all(sending, "expert", split_axis=1, concat_axis=1, tiled=True)
    arrived = arrived.reshape(2, n_experts * half_slots, width)
    gate_w = w_gate[0]
    up_w = w_up[0]
    down_w = w_down[0]
    gate_s = shadow_gate[0]
    up_s = shadow_up[0]
    down_s = shadow_down[0]

    def swiglu(rows, gate_m, up_m):
        gate = jnp.dot(rows, gate_m, preferred_element_type=jnp.float32)
        up = jnp.dot(rows, up_m, preferred_element_type=jnp.float32)
        return (jax.nn.silu(gate) * up).astype(jnp.bfloat16)

    def hidden_rows(piece, start):
        own = swiglu(piece[0], gate_w, up_w)
        other = swiglu(piece[1], gate_s, up_s)
        return jnp.stack([own, other], axis=1)

    hidden = work_in_pieces(arrived, "shard", 1, hidden_rows, 0)
    own = jnp.dot(hidden[:, 0], down_w, preferred_element_type=jnp.float32)
    other = jnp.dot(hidden[:, 1], down_s, preferred_element_type=jnp.float32)
    summed = sum_at_owner(jnp.stack([own, other], axis=1).astype(jnp.bfloat16), "shard", 0)
    finished = summed.astype(jnp.bfloat16).reshape(n_experts, half_slots, 2, width)
    returned = lax.all_to_all(finished, "expert", split_axis=0, concat_axis=0, tiled=True)
    even_back = returned[:, :, 0]
    odd_back = jnp.roll(returned[:, :, 1], 1, axis=0)
    by_expert = jnp.stack([even_back, odd_back], axis=2).reshape(n_experts * slots_per, width)
    picked = (
        by_expert[positions].reshape(local_tokens, expert_ids.shape[1], width).astype(jnp.float32)
    )
    mixed = jnp.sum(gates[:, :, None] * picked, axis=1)
    return mixed.astype(jnp.bfloat16)


def solution(mesh):
    placed = (
        P(("expert", "shard"), None),
        P(),
        P(("expert", "shard"), None),
        P("expert", None, "shard"),
        P("expert", None, "shard"),
        P("expert", "shard", None),
    )
    return jax.shard_map(
        shards, mesh=mesh, in_specs=placed, out_specs=P(("expert", "shard"), None), check_vma=False
    )
```

profile of v0, /device:TPU:1, one launch (start us, length us, event | category | flops | bytes accessed | tf_op | source)
XLA Modules:
  0.0 370.6 jit_solution(15408557589807152107)
XLA Ops:
  6.5 0.7 broadcast_multiply_fusion
  7.3 0.8 copy.103
  8.7 1.2 scatter_custom_fusion
  11.1 12.1 %all_to_all.15 = bf16[2,8,2,4096]{3,2,0,1:T(2,128)(2,1)S(1)} all-to-all(bf16[2,8,2,4096]{3,2,0,1:T(2,128)(2,1)S(1)} %copy.113), channel_id=1, replica_groups=mesh['expert'=8,'shard'=16] {'expert'}, dimensions={1} | all-to-all | bytes 524288 | tf_op jit(solution)/shard_map/all_to_all | solution.py:66
  23.7 0.7 copy.118
  24.6 1.1 collective-permute-start
  25.9 0.7 copy.115
  26.7 1.1 collective-permute-start.2
  27.7 41.2 %all-gather.7.cloned.1.call-done = bf16[32,8,4096]{2,1,0:T(8,128)(2,1)} async-done(((bf16[2,8,4096]{2,1,0:T(8,128)(2,1)}), bf16[32,8,4096]{2,1,0:T(8,128)(2,1)}) %all-gather.7.cloned.1.call-update) | async-done | bytes 2097168 | tf_op jit(solution)/shard_map/all_gather | solution.py:26
  69.0 4.7 %fusion.16 = f32[16,8,896]{2,1,0:T(8,128)S(1)} fusion(bf16[1,4096,896]{2,1,0:T(8,128)(2,1)} %param.9, bf16[16,2,8,4096]{3,2,1,0:T(8,128)(2,1)} %bitcast.140), kind=kOutput, calls=%fused_computation.20 | convolution fusion | flops 939524096 | bytes 8847360 | tf_op jit(solution)/shard_map/vmap()/dot_general | solution.py:76
  73.6 41.8 %all-gather.5.cloned.1.call-done = bf16[32,8,4096]{2,1,0:T(8,128)(2,1)} async-done(((bf16[2,8,4096]{2,1,0:T(8,128)(2,1)}), bf16[32,8,4096]{2,1,0:T(8,128)(2,1)}) %all-gather.5.cloned.1.call-update) | async-done | bytes 2097168 | tf_op jit(solution)/shard_map/all_gather | solution.py:26
  115.4 4.8 %fusion.18 = f32[16,8,896]{2,1,0:T(8,128)S(1)} fusion(bf16[1,4096,896]{2,1,0:T(8,128)(2,1)} %param.9, bf16[16,2,8,4096]{3,2,1,0:T(8,128)(2,1)} %bitcast.144), kind=kOutput, calls=%fused_computation.22 | convolution fusion | flops 939524096 | bytes 8847360 | tf_op jit(solution)/shard_map/vmap()/dot_general | solution.py:76
  120.3 4.5 %fusion.47 = bf16[16,8,1,896]{3,1,0,2:T(8,128)(2,1)S(1)} fusion(bf16[1,4096,896]{2,1,0:T(8,128)(2,1)} %param.10, bf16[16,2,8,4096]{3,2,1,0:T(8,128)(2,1)S(1)} %bitcast.141, f32[16,8,896]{2,1,0:T(8,128)S(1)} %fusion.16), kind=kOutput, calls=%fused_computation.34 | convolution fusion | flops 940212224 | bytes 9076736 | tf_op jit(solution)/shard_map/vmap()/dot_general | solution.py:77
  124.9 1.3 fusion.44
  126.2 4.4 %fusion.8 = f32[16,8,896]{2,1,0:T(8,128)S(1)} fusion(bf16[1,4096,896]{2,1,0:T(8,128)(2,1)} %collective-permute-done, bf16[16,2,8,4096]{3,2,1,0:T(8,128)(2,1)S(1)} %bitcast.142), kind=kOutput, calls=%fused_computation.12 | convolution fusion | flops 939524096 | bytes 8847360 | tf_op jit(solution)/shard_map/vmap()/dot_general | solution.py:76
  130.6 4.4 %fusion.10 = f32[16,8,896]{2,1,0:T(8,128)S(1)} fusion(bf16[1,4096,896]{2,1,0:T(8,128)(2,1)} %collective-permute-done, bf16[16,2,8,4096]{3,2,1,0:T(8,128)(2,1)S(1)} %bitcast.146), kind=kOutput, calls=%fused_computation.14 | convolution fusion | flops 939524096 | bytes 8847360 | tf_op jit(solution)/shard_map/vmap()/dot_general | solution.py:76
  135.0 50.3 %collective-permute-done.1 = bf16[1,4096,896]{2,1,0:T(8,128)(2,1)} collective-permute-done((bf16[1,4096,896]{2,1,0:T(8,128)(2,1)}, bf16[1,4096,896]{2,1,0:T(8,128)(2,1)}, u32[]{:S(2)}, u32[]{:S(2)}) %collective-permute-start.1) | collective-permute-done | bytes 7340064 | tf_op jit(solution)/shard_map/ppermute | solution.py:10
  185.2 4.5 %fusion.51 = bf16[16,8,1,896]{3,1,0,2:T(8,128)(2,1)S(1)} fusion(f32[16,8,896]{2,1,0:T(8,128)S(1)} %fusion.8, bf16[1,4096,896]{2,1,0:T(8,128)(2,1)} %collective-permute-done.1, bf16[16,2,8,4096]{3,2,1,0:T(8,128)(2,1)S(1)} %bitcast.143), kind=kOutput, calls=%fused_computation.46 | convolution fusion | flops 940212224 | bytes 9076736 | tf_op jit(solution)/shard_map/vmap()/dot_general | solution.py:77
  189.8 4.5 %fusion.50 = bf16[16,8,1,896]{3,1,0,2:T(8,128)(2,1)S(1)} fusion(f32[16,8,896]{2,1,0:T(8,128)S(1)} %fusion.10, bf16[1,4096,896]{2,1,0:T(8,128)(2,1)} %collective-permute-done.1, bf16[16,2,8,4096]{3,2,1,0:T(8,128)(2,1)S(1)} %bitcast.147), kind=kOutput, calls=%fused_computation.45 | convolution fusion | flops 940212224 | bytes 9076736 | tf_op jit(solution)/shard_map/vmap()/dot_general | solution.py:77
  194.5 2.6 fusion.29
  197.2 66.7 %collective-permute-done.2 = bf16[1,896,4096]{2,1,0:T(8,128)(2,1)} collective-permute-done((bf16[1,896,4096]{2,1,0:T(8,128)(2,1)}, bf16[1,896,4096]{2,1,0:T(8,128)(2,1)}, u32[]{:S(2)}, u32[]{:S(2)}) %collective-permute-start.2) | collective-permute-done | bytes 7340064 | tf_op jit(solution)/shard_map/ppermute | solution.py:10
  263.9 5.5 %fusion.26 = bf16[16,16,1,4096]{3,1,0,2:T(8,128)(2,1)S(1)} fusion(bf16[16,16,896]{2,1,0:T(8,128)(2,1)S(1)} %bitcast.153, bf16[1,896,4096]{2,1,0:T(8,128)(2,1)} %collective-permute-done.2), kind=kOutput, calls=%fused_computation.26 | convolution fusion | flops 1880096768 | bytes 9895936 | tf_op jit(solution)/shard_map/dot_general | solution.py:87
  269.8 2.2 copy.121
  272.0 8.0 %all-to-all-start.1 = ((bf16[16,16,2,4096]{3,1,2,0:T(8,128)(2,1)}), bf16[16,16,2,4096]{3,1,2,0:T(8,128)(2,1)}, u32[]{:S(2)}, u32[]{:S(2)}) async-start(bf16[16,16,2,4096]{3,1,2,0:T(8,128)(2,1)} %copy.121), calls=%async_computation.1 | async-start | bytes 8388608 | tf_op jit(solution)/shard_map/all_to_all | solution.py:37
  280.4 0.7 gather_fusion.1
  281.2 64.8 %all-to-all-done.1 = bf16[16,16,2,4096]{3,1,2,0:T(8,128)(2,1)} async-done(((bf16[16,16,2,4096]{3,1,2,0:T(8,128)(2,1)}), bf16[16,16,2,4096]{3,1,2,0:T(8,128)(2,1)}, u32[]{:S(2)}, u32[]{:S(2)}) %all-to-all-start.1) | async-done | bytes 4194336 | tf_op jit(solution)/shard_map/all_to_all | solution.py:37
  346.0 3.0 reduce_sum.34
  349.0 1.0 copy.123
  349.9 3.8 %all-to-all-start.2 = ((bf16[8,2,2,4096]{3,2,1,0:T(2,128)(2,1)}), bf16[8,2,2,4096]{3,2,1,0:T(2,128)(2,1)S(1)}, u32[]{:S(2)}, u32[]{:S(2)}) async-start(bf16[8,2,2,4096]{3,2,1,0:T(2,128)(2,1)} %bitcast.36), calls=%async_computation.2 | async-start | bytes 524288 | tf_op jit(solution)/shard_map/all_to_all | solution.py:90
  353.9 6.3 %all-to-all-done.2 = bf16[8,2,2,4096]{3,2,1,0:T(2,128)(2,1)S(1)} async-done(((bf16[8,2,2,4096]{3,2,1,0:T(2,128)(2,1)}), bf16[8,2,2,4096]{3,2,1,0:T(2,128)(2,1)S(1)}, u32[]{:S(2)}, u32[]{:S(2)}) %all-to-all-start.2) | async-done | bytes 262176 | tf_op jit(solution)/shard_map/all_to_all | solution.py:90
  361.9 0.6 gather_fusion
  362.7 1.0 multiply_reduce_fusion
  (68 shorter events, 5.8 us)
Async XLA Ops:
  6.5 2.1 copy-start
  6.5 62.4 %all-gather.7.cloned.1.call-start = ((), (), s32[]{:S(2)}) async-start(), calls=%async_computation.4 | async-start | bytes 2228224 | tf_op jit(solution)/shard_map/all_gather | solution.py:26
  24.4 91.0 %all-gather.5.cloned.1.call-start = ((), (), s32[]{:S(2)}) async-start(), calls=%async_computation.3 | async-start | bytes 2228224 | tf_op jit(solution)/shard_map/all_gather | solution.py:26
  24.6 101.6 %collective-permute-start = (bf16[1,4096,896]{2,1,0:T(8,128)(2,1)}, bf16[1,4096,896]{2,1,0:T(8,128)(2,1)}, u32[]{:S(2)}, u32[]{:S(2)}) collective-permute-start(bf16[1,4096,896]{2,1,0:T(8,128)(2,1)} %param.9), channel_id=1, source_target_pairs={{0,112},{16,0},{32,16},{48,32},{64,48},{80,64},{96,80},{112,96},{1... | collective-permute-start | bytes 22020104 | tf_op jit(solution)/shard_map/ppermute | solution.py:10
  25.7 159.6 %collective-permute-start.1 = (bf16[1,4096,896]{2,1,0:T(8,128)(2,1)}, bf16[1,4096,896]{2,1,0:T(8,128)(2,1)}, u32[]{:S(2)}, u32[]{:S(2)}) collective-permute-start(bf16[1,4096,896]{2,1,0:T(8,128)(2,1)} %param.10), channel_id=1, source_target_pairs={{0,112},{16,0},{32,16},{48,32},{64,48},{80,64},{96,80},{112,96},{1... | collective-permute-start | bytes 22020104 | tf_op jit(solution)/shard_map/ppermute | solution.py:10
  26.7 237.2 %collective-permute-start.2 = (bf16[1,896,4096]{2,1,0:T(8,128)(2,1)}, bf16[1,896,4096]{2,1,0:T(8,128)(2,1)}, u32[]{:S(2)}, u32[]{:S(2)}) collective-permute-start(bf16[1,896,4096]{2,1,0:T(8,128)(2,1)} %param.11), channel_id=1, source_target_pairs={{0,112},{16,0},{32,16},{48,32},{64,48},{80,64},{96,80},{112,96},{1... | collective-permute-start | bytes 22020104 | tf_op jit(solution)/shard_map/ppermute | solution.py:10
  115.4 4.8 %copy-start.1 = (bf16[32,8,4096]{2,1,0:T(8,128)(2,1)S(1)}, bf16[32,8,4096]{2,1,0:T(8,128)(2,1)}, u32[]{:S(2)}) copy-start(bf16[32,8,4096]{2,1,0:T(8,128)(2,1)} %all-gather.7.cloned.1.call-done) | copy-start | bytes 6291460
  115.4 9.4 %slice-start = ((s8[7340032]{0:T(1024)(128)(4,1)}), s8[4194304]{0:T(1024)(128)(4,1)S(1)}, s32[]{:S(2)}) async-start(s8[7340032]{0:T(1024)(128)(4,1)} %bitcast.157), calls=%async_computation.5 | async-start | bytes 8388608
  120.2 4.6 %copy-start.2 = (bf16[32,8,4096]{2,1,0:T(8,128)(2,1)S(1)}, bf16[32,8,4096]{2,1,0:T(8,128)(2,1)}, u32[]{:S(2)}) copy-start(bf16[32,8,4096]{2,1,0:T(8,128)(2,1)} %all-gather.5.cloned.1.call-done) | copy-start | bytes 6291460
  120.2 4.7 %slice-start.1 = ((s8[7340032]{0:T(1024)(128)(4,1)}), s8[3145728]{0:T(1024)(128)(4,1)S(1)}, s32[]{:S(2)}) async-start(s8[7340032]{0:T(1024)(128)(4,1)} %bitcast.157), calls=%async_computation.6 | async-start | bytes 6291456
  185.2 9.3 %slice-start.2 = ((s8[7340032]{0:T(1024)(128)(4,1)}), s8[4194304]{0:T(1024)(128)(4,1)S(1)}, s32[]{:S(2)}) async-start(s8[7340032]{0:T(1024)(128)(4,1)} %bitcast.159), calls=%async_computation.7 | async-start | bytes 8388608
  189.8 4.7 %slice-start.3 = ((s8[7340032]{0:T(1024)(128)(4,1)}), s8[3145728]{0:T(1024)(128)(4,1)S(1)}, s32[]{:S(2)}) async-start(s8[7340032]{0:T(1024)(128)(4,1)} %bitcast.159), calls=%async_computation.8 | async-start | bytes 6291456
  272.0 8.2 %copy-start.3 = (bf16[4096,8]{0,1:T(8,128)(2,1)S(1)}, bf16[4096,8]{0,1:T(8,128)(2,1)}, u32[]{:S(2)}) copy-start(bf16[4096,8]{0,1:T(8,128)(2,1)} %param.7) | copy-start | bytes 196612
  272.0 74.0 %all-to-all-start.1 = ((bf16[16,16,2,4096]{3,1,2,0:T(8,128)(2,1)}), bf16[16,16,2,4096]{3,1,2,0:T(8,128)(2,1)}, u32[]{:S(2)}, u32[]{:S(2)}) async-start(bf16[16,16,2,4096]{3,1,2,0:T(8,128)(2,1)} %copy.121), calls=%async_computation.1 | async-start | bytes 8388608 | tf_op jit(solution)/shard_map/all_to_all | solution.py:37
  349.9 10.3 %all-to-all-start.2 = ((bf16[8,2,2,4096]{3,2,1,0:T(2,128)(2,1)}), bf16[8,2,2,4096]{3,2,1,0:T(2,128)(2,1)S(1)}, u32[]{:S(2)}, u32[]{:S(2)}) async-start(bf16[8,2,2,4096]{3,2,1,0:T(2,128)(2,1)} %bitcast.36), calls=%async_computation.2 | async-start | bytes 524288 | tf_op jit(solution)/shard_map/all_to_all | solution.py:90
Sparse Core Ops, SparseCore 0:
  24.5 44.3 all-gather.6
  71.1 44.2 all-gather.4
where the time goes:
time: 371 us
  waiting for transfers between devices  271 us (73%)
  matrix products  41.4 us (11%)
  starting transfers between devices  14.3 us (4%)
  between operations  13.8 us (4%)
  blocking collectives  12.1 us (3%)
  local copies, waits for them, and re-layouts  11.3 us (3%)
  other arithmetic  6.56 us (2%)
    ppermute x3, waiting for transfers between devices, from_behind(): return lax.ppermute(value, axis, pairs)  117 us
    all_gather x2, waiting for transfers between devices, work_in_pieces(): gathered.append(jax.vmap(apply)(lax.all_gather(share, axis), starts))  83 us
    all_to_all x1, waiting for transfers between devices, sum_at_owner(): blocks = lax.all_to_all(split_up(x, dim, devices), axis, 0, 0, tiled=True)  64.8 us
    dot_general x4, matrix products, swiglu(): gate = jnp.dot(rows, gate_m, preferred_element_type=jnp.float32)  18.2 us
    dot_general x4, matrix products, swiglu(): up = jnp.dot(rows, up_m, preferred_element_type=jnp.float32)  14.9 us
    all_to_all x1, blocking collectives, shards(): lax.all_to_all(sending, 'expert', split_axis=1, concat_axis=1, tiled=True)  12.1 us
    all_to_all x1, starting transfers between devices, sum_at_owner(): blocks = lax.all_to_all(split_up(x, dim, devices), axis, 0, 0, tiled=True)  7.95 us
  transfers between devices with their start and end apart: 7, of which 6 were waited for; matrix products, arithmetic and copies ran while one was open for 10% of the time, Pallas kernels for 0%

commit v1 on v0

--- a/solution.py
+++ b/solution.py
@@ -63,7 +63,12 @@
     even_rows = outgoing[:, :, 0]
     odd_rows = jnp.roll(outgoing[:, :, 1], -1, axis=0)
     sending = jnp.stack([even_rows, odd_rows], axis=0)
-    arrived = lax.all_to_all(sending, "expert", split_axis=1, concat_axis=1, tiled=True)
+    arrived = jnp.concatenate(
+        lax.all_to_all(
+            jnp.stack(jnp.split(sending, lax.axis_size("expert"), axis=1)), "expert", 0, 0
+        ),
+        axis=1,
+    )
     arrived = arrived.reshape(2, n_experts * half_slots, width)
     gate_w = w_gate[0]
     up_w = w_up[0]

time: 371 us -> 372 us (level)
  no operation moved by 1% of the time
where the time goes in v1:
time: 372 us; the launch traced here: 371 us
  waiting for transfers between devices  271 us (73%)
  matrix products  41.4 us (11%)
  starting transfers between devices  14.3 us (4%)
  between operations  13.8 us (4%)
  blocking collectives  12.1 us (3%)
  local copies, waits for them, and re-layouts  11.5 us (3%)
  other arithmetic  7.11 us (2%)
    ppermute x3, waiting for transfers between devices, from_behind(): return lax.ppermute(value, axis, pairs)  117 us
    all_gather x2, waiting for transfers between devices, work_in_pieces(): gathered.append(jax.vmap(apply)(lax.all_gather(share, axis), starts))  83 us
    all_to_all x1, waiting for transfers between devices, sum_at_owner(): blocks = lax.all_to_all(split_up(x, dim, devices), axis, 0, 0, tiled=True)  64.8 us
    dot_general x4, matrix products, swiglu(): gate = jnp.dot(rows, gate_m, preferred_element_type=jnp.float32)  18.2 us
    dot_general x4, matrix products, swiglu(): up = jnp.dot(rows, up_m, preferred_element_type=jnp.float32)  14.9 us
    all_to_all x1, blocking collectives, shards(): lax.all_to_all(jnp.stack(jnp.split(sending, lax.axis_size('expert'), axis...  12.1 us
    all_to_all x1, starting transfers between devices, sum_at_owner(): blocks = lax.all_to_all(split_up(x, dim, devices), axis, 0, 0, tiled=True)  7.95 us
  transfers between devices with their start and end apart: 7, of which 6 were waited for; matrix products, arithmetic and copies ran while one was open for 10% of the time, Pallas kernels for 0%

profile of v1, /device:TPU:1, one launch (start us, length us, event | category | flops | bytes accessed | tf_op | source)
XLA Modules:
  0.0 371.4 jit_solution(15291652771396892532)
XLA Ops:
  6.5 0.7 broadcast_multiply_fusion
  7.3 0.8 copy.293
  8.7 1.2 scatter_custom_fusion
  11.9 12.1 %all_to_all.15 = bf16[8,2,1,2,4096]{4,3,1,2,0:T(2,128)(2,1)S(1)} all-to-all(bf16[8,2,1,2,4096]{4,3,1,2,0:T(2,128)(2,1)S(1)} %bitcast_dynamic-update-slice_fusion), channel_id=1, replica_groups=mesh['expert'=8,'shard'=16] {'expert'}, dimensions={0} | all-to-all | bytes 524288 | tf_op jit(solution)/shard_map/all_to_all | solution.py:67
  24.4 0.7 copy.307
  25.4 1.1 collective-permute-start
  26.7 0.7 copy.304
  27.5 1.1 collective-permute-start.2
  28.5 41.2 %all-gather.7.cloned.1.call-done = bf16[32,8,4096]{2,1,0:T(8,128)(2,1)} async-done(((bf16[2,8,4096]{2,1,0:T(8,128)(2,1)}), bf16[32,8,4096]{2,1,0:T(8,128)(2,1)}) %all-gather.7.cloned.1.call-update) | async-done | bytes 2097168 | tf_op jit(solution)/shard_map/all_gather | solution.py:26
  69.8 4.7 %fusion.16 = f32[16,8,896]{2,1,0:T(8,128)S(1)} fusion(bf16[1,4096,896]{2,1,0:T(8,128)(2,1)} %param.9, bf16[16,2,8,4096]{3,2,1,0:T(8,128)(2,1)} %bitcast.157), kind=kOutput, calls=%fused_computation.20 | convolution fusion | flops 939524096 | bytes 8847360 | tf_op jit(solution)/shard_map/vmap()/dot_general | solution.py:81
  74.4 41.8 %all-gather.5.cloned.1.call-done = bf16[32,8,4096]{2,1,0:T(8,128)(2,1)} async-done(((bf16[2,8,4096]{2,1,0:T(8,128)(2,1)}), bf16[32,8,4096]{2,1,0:T(8,128)(2,1)}) %all-gather.5.cloned.1.call-update) | async-done | bytes 2097168 | tf_op jit(solution)/shard_map/all_gather | solution.py:26
  116.2 4.8 %fusion.18 = f32[16,8,896]{2,1,0:T(8,128)S(1)} fusion(bf16[1,4096,896]{2,1,0:T(8,128)(2,1)} %param.9, bf16[16,2,8,4096]{3,2,1,0:T(8,128)(2,1)} %bitcast.161), kind=kOutput, calls=%fused_computation.22 | convolution fusion | flops 939524096 | bytes 8847360 | tf_op jit(solution)/shard_map/vmap()/dot_general | solution.py:81
  121.1 4.5 %fusion.47 = bf16[16,8,1,896]{3,1,0,2:T(8,128)(2,1)S(1)} fusion(bf16[1,4096,896]{2,1,0:T(8,128)(2,1)} %param.10, bf16[16,2,8,4096]{3,2,1,0:T(8,128)(2,1)S(1)} %bitcast.158, f32[16,8,896]{2,1,0:T(8,128)S(1)} %fusion.16), kind=kOutput, calls=%fused_computation.34 | convolution fusion | flops 940212224 | bytes 9076736 | tf_op jit(solution)/shard_map/vmap()/dot_general | solution.py:82
  125.7 1.3 fusion.44
  127.0 4.4 %fusion.8 = f32[16,8,896]{2,1,0:T(8,128)S(1)} fusion(bf16[1,4096,896]{2,1,0:T(8,128)(2,1)} %collective-permute-done, bf16[16,2,8,4096]{3,2,1,0:T(8,128)(2,1)S(1)} %bitcast.159), kind=kOutput, calls=%fused_computation.12 | convolution fusion | flops 939524096 | bytes 8847360 | tf_op jit(solution)/shard_map/vmap()/dot_general | solution.py:81
  131.4 4.4 %fusion.10 = f32[16,8,896]{2,1,0:T(8,128)S(1)} fusion(bf16[1,4096,896]{2,1,0:T(8,128)(2,1)} %collective-permute-done, bf16[16,2,8,4096]{3,2,1,0:T(8,128)(2,1)S(1)} %bitcast.163), kind=kOutput, calls=%fused_computation.14 | convolution fusion | flops 939524096 | bytes 8847360 | tf_op jit(solution)/shard_map/vmap()/dot_general | solution.py:81
  135.8 50.3 %collective-permute-done.1 = bf16[1,4096,896]{2,1,0:T(8,128)(2,1)} collective-permute-done((bf16[1,4096,896]{2,1,0:T(8,128)(2,1)}, bf16[1,4096,896]{2,1,0:T(8,128)(2,1)}, u32[]{:S(2)}, u32[]{:S(2)}) %collective-permute-start.1) | collective-permute-done | bytes 7340064 | tf_op jit(solution)/shard_map/ppermute | solution.py:10
  186.0 4.5 %fusion.51 = bf16[16,8,1,896]{3,1,0,2:T(8,128)(2,1)S(1)} fusion(f32[16,8,896]{2,1,0:T(8,128)S(1)} %fusion.8, bf16[1,4096,896]{2,1,0:T(8,128)(2,1)} %collective-permute-done.1, bf16[16,2,8,4096]{3,2,1,0:T(8,128)(2,1)S(1)} %bitcast.160), kind=kOutput, calls=%fused_computation.59 | convolution fusion | flops 940212224 | bytes 9076736 | tf_op jit(solution)/shard_map/vmap()/dot_general | solution.py:82
  190.6 4.5 %fusion.50 = bf16[16,8,1,896]{3,1,0,2:T(8,128)(2,1)S(1)} fusion(f32[16,8,896]{2,1,0:T(8,128)S(1)} %fusion.10, bf16[1,4096,896]{2,1,0:T(8,128)(2,1)} %collective-permute-done.1, bf16[16,2,8,4096]{3,2,1,0:T(8,128)(2,1)S(1)} %bitcast.164), kind=kOutput, calls=%fused_computation.58 | convolution fusion | flops 940212224 | bytes 9076736 | tf_op jit(solution)/shard_map/vmap()/dot_general | solution.py:82
  195.3 2.6 fusion.29
  198.0 66.7 %collective-permute-done.2 = bf16[1,896,4096]{2,1,0:T(8,128)(2,1)} collective-permute-done((bf16[1,896,4096]{2,1,0:T(8,128)(2,1)}, bf16[1,896,4096]{2,1,0:T(8,128)(2,1)}, u32[]{:S(2)}, u32[]{:S(2)}) %collective-permute-start.2) | collective-permute-done | bytes 7340064 | tf_op jit(solution)/shard_map/ppermute | solution.py:10
  264.7 5.5 %fusion.26 = bf16[16,16,1,4096]{3,1,0,2:T(8,128)(2,1)S(1)} fusion(bf16[16,16,896]{2,1,0:T(8,128)(2,1)S(1)} %bitcast.171, bf16[1,896,4096]{2,1,0:T(8,128)(2,1)} %collective-permute-done.2), kind=kOutput, calls=%fused_computation.26 | convolution fusion | flops 1880096768 | bytes 9895936 | tf_op jit(solution)/shard_map/dot_general | solution.py:92
  270.6 2.3 copy.310
  272.8 8.0 %all-to-all-start.1 = ((bf16[16,16,2,4096]{3,1,2,0:T(8,128)(2,1)}), bf16[16,16,2,4096]{3,1,2,0:T(8,128)(2,1)}, u32[]{:S(2)}, u32[]{:S(2)}) async-start(bf16[16,16,2,4096]{3,1,2,0:T(8,128)(2,1)} %copy.310), calls=%async_computation.1 | async-start | bytes 8388608 | tf_op jit(solution)/shard_map/all_to_all | solution.py:37
  281.2 0.7 gather_fusion.1
  282.0 64.8 %all-to-all-done.1 = bf16[16,16,2,4096]{3,1,2,0:T(8,128)(2,1)} async-done(((bf16[16,16,2,4096]{3,1,2,0:T(8,128)(2,1)}), bf16[16,16,2,4096]{3,1,2,0:T(8,128)(2,1)}, u32[]{:S(2)}, u32[]{:S(2)}) %all-to-all-start.1) | async-done | bytes 4194336 | tf_op jit(solution)/shard_map/all_to_all | solution.py:37
  346.8 3.0 reduce_sum.34
  349.8 1.0 copy.312
  350.8 3.8 %all-to-all-start.2 = ((bf16[8,2,2,4096]{3,2,1,0:T(2,128)(2,1)}), bf16[8,2,2,4096]{3,2,1,0:T(2,128)(2,1)S(1)}, u32[]{:S(2)}, u32[]{:S(2)}) async-start(bf16[8,2,2,4096]{3,2,1,0:T(2,128)(2,1)} %bitcast.37), calls=%async_computation.2 | async-start | bytes 524288 | tf_op jit(solution)/shard_map/all_to_all | solution.py:95
  354.7 6.3 %all-to-all-done.2 = bf16[8,2,2,4096]{3,2,1,0:T(2,128)(2,1)S(1)} async-done(((bf16[8,2,2,4096]{3,2,1,0:T(2,128)(2,1)}), bf16[8,2,2,4096]{3,2,1,0:T(2,128)(2,1)S(1)}, u32[]{:S(2)}, u32[]{:S(2)}) %all-to-all-start.2) | async-done | bytes 262176 | tf_op jit(solution)/shard_map/all_to_all | solution.py:95
  362.7 0.6 gather_fusion
  363.6 1.0 multiply_reduce_fusion
  (74 shorter events, 6.6 us)
Async XLA Ops:
  6.5 2.1 copy-start
  6.5 63.2 %all-gather.7.cloned.1.call-start = ((), (), s32[]{:S(2)}) async-start(), calls=%async_computation.4 | async-start | bytes 2228224 | tf_op jit(solution)/shard_map/all_gather | solution.py:26
  25.2 91.0 %all-gather.5.cloned.1.call-start = ((), (), s32[]{:S(2)}) async-start(), calls=%async_computation.3 | async-start | bytes 2228224 | tf_op jit(solution)/shard_map/all_gather | solution.py:26
  25.4 101.6 %collective-permute-start = (bf16[1,4096,896]{2,1,0:T(8,128)(2,1)}, bf16[1,4096,896]{2,1,0:T(8,128)(2,1)}, u32[]{:S(2)}, u32[]{:S(2)}) collective-permute-start(bf16[1,4096,896]{2,1,0:T(8,128)(2,1)} %param.9), channel_id=1, source_target_pairs={{0,112},{16,0},{32,16},{48,32},{64,48},{80,64},{96,80},{112,96},{1... | collective-permute-start | bytes 22020104 | tf_op jit(solution)/shard_map/ppermute | solution.py:10
  26.5 159.6 %collective-permute-start.1 = (bf16[1,4096,896]{2,1,0:T(8,128)(2,1)}, bf16[1,4096,896]{2,1,0:T(8,128)(2,1)}, u32[]{:S(2)}, u32[]{:S(2)}) collective-permute-start(bf16[1,4096,896]{2,1,0:T(8,128)(2,1)} %param.10), channel_id=1, source_target_pairs={{0,112},{16,0},{32,16},{48,32},{64,48},{80,64},{96,80},{112,96},{1... | collective-permute-start | bytes 22020104 | tf_op jit(solution)/shard_map/ppermute | solution.py:10
  27.5 237.2 %collective-permute-start.2 = (bf16[1,896,4096]{2,1,0:T(8,128)(2,1)}, bf16[1,896,4096]{2,1,0:T(8,128)(2,1)}, u32[]{:S(2)}, u32[]{:S(2)}) collective-permute-start(bf16[1,896,4096]{2,1,0:T(8,128)(2,1)} %param.11), channel_id=1, source_target_pairs={{0,112},{16,0},{32,16},{48,32},{64,48},{80,64},{96,80},{112,96},{1... | collective-permute-start | bytes 22020104 | tf_op jit(solution)/shard_map/ppermute | solution.py:10
  116.2 4.8 %copy-start.1 = (bf16[32,8,4096]{2,1,0:T(8,128)(2,1)S(1)}, bf16[32,8,4096]{2,1,0:T(8,128)(2,1)}, u32[]{:S(2)}) copy-start(bf16[32,8,4096]{2,1,0:T(8,128)(2,1)} %all-gather.7.cloned.1.call-done) | copy-start | bytes 6291460
  116.2 9.4 %slice-start = ((s8[7340032]{0:T(1024)(128)(4,1)}), s8[4194304]{0:T(1024)(128)(4,1)S(1)}, s32[]{:S(2)}) async-start(s8[7340032]{0:T(1024)(128)(4,1)} %bitcast.175), calls=%async_computation.5 | async-start | bytes 8388608
  121.0 4.6 %copy-start.2 = (bf16[32,8,4096]{2,1,0:T(8,128)(2,1)S(1)}, bf16[32,8,4096]{2,1,0:T(8,128)(2,1)}, u32[]{:S(2)}) copy-start(bf16[32,8,4096]{2,1,0:T(8,128)(2,1)} %all-gather.5.cloned.1.call-done) | copy-start | bytes 6291460
  121.0 4.7 %slice-start.1 = ((s8[7340032]{0:T(1024)(128)(4,1)}), s8[3145728]{0:T(1024)(128)(4,1)S(1)}, s32[]{:S(2)}) async-start(s8[7340032]{0:T(1024)(128)(4,1)} %bitcast.175), calls=%async_computation.6 | async-start | bytes 6291456
  186.0 9.3 %slice-start.2 = ((s8[7340032]{0:T(1024)(128)(4,1)}), s8[4194304]{0:T(1024)(128)(4,1)S(1)}, s32[]{:S(2)}) async-start(s8[7340032]{0:T(1024)(128)(4,1)} %bitcast.177), calls=%async_computation.7 | async-start | bytes 8388608
  190.6 4.7 %slice-start.3 = ((s8[7340032]{0:T(1024)(128)(4,1)}), s8[3145728]{0:T(1024)(128)(4,1)S(1)}, s32[]{:S(2)}) async-start(s8[7340032]{0:T(1024)(128)(4,1)} %bitcast.177), calls=%async_computation.8 | async-start | bytes 6291456
  272.8 8.2 %copy-start.3 = (bf16[4096,8]{0,1:T(8,128)(2,1)S(1)}, bf16[4096,8]{0,1:T(8,128)(2,1)}, u32[]{:S(2)}) copy-start(bf16[4096,8]{0,1:T(8,128)(2,1)} %param.7) | copy-start | bytes 196612
  272.8 74.0 %all-to-all-start.1 = ((bf16[16,16,2,4096]{3,1,2,0:T(8,128)(2,1)}), bf16[16,16,2,4096]{3,1,2,0:T(8,128)(2,1)}, u32[]{:S(2)}, u32[]{:S(2)}) async-start(bf16[16,16,2,4096]{3,1,2,0:T(8,128)(2,1)} %copy.310), calls=%async_computation.1 | async-start | bytes 8388608 | tf_op jit(solution)/shard_map/all_to_all | solution.py:37
  350.8 10.3 %all-to-all-start.2 = ((bf16[8,2,2,4096]{3,2,1,0:T(2,128)(2,1)}), bf16[8,2,2,4096]{3,2,1,0:T(2,128)(2,1)S(1)}, u32[]{:S(2)}, u32[]{:S(2)}) async-start(bf16[8,2,2,4096]{3,2,1,0:T(2,128)(2,1)} %bitcast.37), calls=%async_computation.2 | async-start | bytes 524288 | tf_op jit(solution)/shard_map/all_to_all | solution.py:95
Sparse Core Ops, SparseCore 0:
  25.3 44.3 all-gather.6
  71.9 44.2 all-gather.4
